TPU v7x, 32 devices: a whole 2x2x4 slice. The times are simulated.
32 devices in a mesh: ga: 2 (over core), band: 16 (over z, y, x).
Axes of the slice: x: 2, y: 2, z: 4, core: 2. Of those that a mesh axis runs over, the one named last changes fastest.
Arguments:
- orbitals: bfloat16 [1024, 2, 16384], P('band', None, 'ga'), may hold values from -6 to 6
- projectors: bfloat16 [864, 2, 16384], P(None, None, ('ga', 'band')), may hold values from -0.03125 to 0.03125
- coupling: float32 [4, 18, 18], replicated, may hold values from -6 to 6
- species: int32 [48], replicated, may hold values from 0 to 3
- offsets: int32 [48], replicated, may hold values from 0 to 846, as said below
Outputs:
- applied: bfloat16 [1024, 2, 16384], P('band', None, 'ga')
Inputs may be any that keep to these rules, and one draw needn't show every extreme that they name: Each atom's 18 projectors are the 18 consecutive rows of projectors starting at its offset; offsets are multiples of 18, and the atoms' blocks are distinct and cover all 864 rows.
All inputs are finite; a program needn't handle non-finite values.
Results may differ from a plain program's by a relative error of at most 0.0049.
Values may be sent and summed in bfloat16 or wider, within the bound.
A program may use at most 64 MiB of HBM per device.

v0:
```python
import functools

import jax
import jax.numpy as jnp
import numpy as np
from jax import lax
from jax.experimental import pallas as pl
from jax.experimental.pallas import tpu as pltpu
from jax.sharding import PartitionSpec as P

MESH = pl.DeviceIdType.MESH
INNER = 4
F32 = jnp.float32
BF16 = jnp.bfloat16


def coupling_rows(coupling, species, offsets, total_proj):
    kinds, per_atom = coupling.shape[0], coupling.shape[1]
    column = jnp.arange(total_proj, dtype=jnp.int32)
    within = column % per_atom
    start = column - within
    kind = jnp.sum(
        jnp.where(offsets[:, None] == start[None, :], species[:, None], 0), axis=0
    )
    pick = (jnp.arange(kinds * per_atom, dtype=jnp.int32)[:, None] == (kind * per_atom + within)[None, :])
    table = jnp.transpose(coupling, (2, 0, 1)).reshape(per_atom, kinds * per_atom)
    return jnp.dot(table, pick.astype(F32), precision=lax.Precision.HIGHEST, preferred_element_type=F32)


def block_diagonal(rows, spread, start_col, start_row):
    full = lax.dot_general(
        spread, rows, (((1,), (0,)), ((), ())), precision=lax.Precision.HIGHEST, preferred_element_type=F32
    )
    return jnp.where(start_col == start_row, full, 0.0)


def block_maps(count, per_atom):
    index = np.arange(count)
    spread = (index[:, None] % per_atom == np.arange(per_atom)[None, :]).astype(np.float32)
    start = (index // per_atom).astype(np.int32)
    return spread, start[:, None], start[None, :]


def dot_t(a, b):
    return lax.dot_general(a, b, (((1,), (1,)), ((), ())), preferred_element_type=F32)


def dot(a, b):
    return lax.dot_general(a, b, (((1,), (0,)), ((), ())), preferred_element_type=F32)


def kernel(
    outer, groups, o_ref, p_ref, rows_ref, spread_ref, col_ref, row_ref, out_ref,
    obuf, pbuf, acc, gsend, grecv, zsend, zrecv, dbuf, rbuf, mbuf,
    o_send, o_recv, p_send, p_recv, l_sem, g_send, g_recv, z_send, z_recv,
    d_send, d_recv, f_send, f_recv, r_send, r_recv, q_sem,
):
    parts = p_ref.shape[1]
    g = lax.axis_index("ga")
    me = lax.axis_index("band")
    o = me // INNER
    n = me % INNER
    bands = o_ref.shape[1]
    wide = p_ref.shape[3]
    span = INNER * wide
    rows = bands // groups
    other = 1 - g
    n1 = n + 1 - 2 * (n % 2)
    n2 = n + 2 - 4 * (n // 2)
    n3 = 3 - n

    def peer(d):
        return (o + d) % outer

    def at_outer(d):
        return {"band": peer(d) * INNER + n}

    side_x = {"band": o * INNER + n1}
    side_y = {"band": o * INNER + n2}
    twin = {"ga": other}

    barrier = pltpu.get_barrier_semaphore()
    partners = [at_outer(d) for d in range(1, outer)] + [side_x, side_y, twin]
    for partner in partners:
        pl.semaphore_signal(barrier, inc=1, device_id=partner, device_id_type=MESH)
    pl.semaphore_wait(barrier, len(partners))

    def remote(src, dst, send, recv, to):
        return pltpu.make_async_remote_copy(
            src_ref=src, dst_ref=dst, send_sem=send, recv_sem=recv, device_id=to, device_id_type=MESH
        )

    mine = pl.ds(pl.multiple_of(o * bands, bands), bands)
    o_copies = []
    for d in range(1, outer):
        src = o_ref.at[:, :, pl.ds(pl.multiple_of(peer(d) * span, span), span)]
        o_copies.append(remote(src, obuf.at[:, mine, :], o_send.at[d], o_recv.at[d], at_outer(d)))
    px, py, fx, fy = {}, {}, {}, {}

    def p_remote(src, slot, c, h, index, to):
        return remote(src, pbuf.at[slot, h, c], p_send.at[h, index], p_recv.at[h, index], to)

    def send_own(h):
        for c in range(2):
            px[h, c] = p_remote(p_ref.at[c, h], n, c, h, c, side_x)
            py[h, c] = p_remote(p_ref.at[c, h], n, c, h, 2 + c, side_y)
        for copy in (px[h, 0], py[h, 1], px[h, 1], py[h, 0]):
            copy.start()

    send_own(0)
    for copy in o_copies:
        copy.start()
    local = [
        pltpu.make_async_copy(
            o_ref.at[:, :, pl.ds(pl.multiple_of(o * span, span), span)], obuf.at[:, mine, :], l_sem.at[0, 0]
        )
    ]
    for h in range(parts):
        for c in range(2):
            local.append(pltpu.make_async_copy(p_ref.at[c, h], pbuf.at[n, h, c], l_sem.at[1 + h, c]))
    for copy in local:
        copy.start()

    for h in range(parts):
        px[h, 0].wait_recv()
        fy[h] = p_remote(pbuf.at[n1, h, 0], n1, 0, h, 4, side_y)
        fy[h].start()
        py[h, 1].wait_recv()
        fx[h] = p_remote(pbuf.at[n2, h, 1], n2, 1, h, 5, side_x)
        fx[h].start()
        if h < parts - 1:
            send_own(h + 1)
        mbuf[h] = block_diagonal(rows_ref[h], spread_ref[...], col_ref[...], row_ref[...])

    for copy in local:
        copy.wait()
    for copy in o_copies:
        copy.wait_recv()

    def project(h):
        def step(slot, carry):
            cols = pl.ds(pl.multiple_of(slot * wide, wide), wide)
            o_real, o_imag = obuf[0, :, cols], obuf[1, :, cols]
            p_real, p_imag = pbuf[slot, h, 0], pbuf[slot, h, 1]
            acc[h, 0] += dot_t(o_real, p_real) + dot_t(o_imag, p_imag)
            acc[h, 1] += dot_t(o_imag, p_real) - dot_t(o_real, p_imag)
            return carry

        px[h, 1].wait_recv()
        py[h, 0].wait_recv()
        fy[h].wait_recv()
        fx[h].wait_recv()
        acc[h] = jnp.zeros_like(acc[h])
        lax.fori_loop(0, INNER, step, 0)

    def piece(position, core):
        return pl.ds(pl.multiple_of(position * bands + core * rows, rows), rows)

    order = list(range(1, outer)) + [0]
    g_copies, z_copies, d_copies, f_copies = {}, {}, {}, {}

    def to_twin(h):
        for d in order:
            gsend[h, d] = acc[h, :, piece(peer(d), other), :]
            g_copies[h, d] = remote(gsend.at[h, d], grecv.at[h, d], g_send.at[h, d], g_recv.at[h, d], twin)
            g_copies[h, d].start()

    def to_outer(h):
        for d in order:
            g_copies[h, d].wait_recv()
            if d:
                zsend[h, d] = (acc[h, :, piece(peer(d), g), :] + grecv[h, d]).astype(BF16)
                z_copies[h, d] = remote(
                    zsend.at[h, d], zrecv.at[h, d], z_send.at[h, d], z_recv.at[h, d], at_outer(d)
                )
                z_copies[h, d].start()

    def couple(h):
        total = acc[h, :, piece(o, g), :] + grecv[h, 0]
        for d in range(1, outer):
            z_copies[h, d].wait_recv()
            total = total + zrecv[h, d].astype(F32)
        for c in range(2):
            coupled = lax.dot_general(
                total[c], mbuf[h], (((1,), (0,)), ((), ())),
                precision=lax.Precision.HIGHEST, preferred_element_type=F32,
            )
            dbuf[h, c, piece(o, g), :] = coupled.astype(BF16)
        own = dbuf.at[h, :, piece(o, g), :]
        for d in range(1, outer):
            d_copies[h, d] = remote(own, own, d_send.at[h, d], d_recv.at[h, d], at_outer(d))
            d_copies[h, d].start()
        f_copies[h, 0] = remote(own, own, f_send.at[h, 0], f_recv.at[h, 0], twin)
        f_copies[h, 0].start()

    def hand_on(h):
        for d in range(1, outer):
            d_copies[h, d].wait_recv()
            got = dbuf.at[h, :, piece(peer(outer - d), g), :]
            f_copies[h, d] = remote(got, got, f_send.at[h, d], f_recv.at[h, d], twin)
            f_copies[h, d].start()

    for h in range(parts - 1):
        project(h)
        to_twin(h)
    for h in range(parts - 1):
        to_outer(h)
    project(parts - 1)
    to_twin(parts - 1)
    to_outer(parts - 1)
    for h in range(parts):
        couple(h)
    for h in range(parts):
        hand_on(h)
    for copy in f_copies.values():
        copy.wait_recv()

    def back(k, d):
        cols = pl.ds(pl.multiple_of((o * INNER + k) * wide, wide), wide)
        src = rbuf.at[k, :, pl.ds(pl.multiple_of(peer(d) * bands, bands), bands), :]
        if d == 0:
            return pltpu.make_async_copy(src, out_ref.at[:, :, cols], q_sem.at[k])
        return remote(src, out_ref.at[:, :, cols], r_send.at[k, d], r_recv.at[k, d], at_outer(d))

    def add_back(k, carry):
        real = imag = 0.0
        for h in range(parts):
            d_real, d_imag = dbuf[h, 0], dbuf[h, 1]
            p_real, p_imag = pbuf[k, h, 0], pbuf[k, h, 1]
            real += dot(d_real, p_real) - dot(d_imag, p_imag)
            imag += dot(d_real, p_imag) + dot(d_imag, p_real)
        rbuf[k, 0] = real.astype(BF16)
        rbuf[k, 1] = imag.astype(BF16)
        for d in order:
            back(k, d).start()
        return carry

    lax.fori_loop(0, INNER, add_back, 0)

    for copy in o_copies:
        copy.wait_send()
    for copies in (px, py, fx, fy, g_copies, z_copies, d_copies, f_copies):
        for copy in copies.values():
            copy.wait_send()

    def finish(k, carry):
        for d in order:
            back(k, d).wait()
        return carry

    lax.fori_loop(0, INNER, finish, 0)


def fused(outer, groups, parts, orbitals, projectors, rows, maps):
    _, bands, reach = orbitals.shape
    _, _, part, wide = projectors.shape
    height = outer * bands
    piece = (parts, outer, 2, bands // groups, part)
    dma = pltpu.SemaphoreType.DMA
    hbm = pl.BlockSpec(memory_space=pl.ANY)
    flops = 16 * height * parts * part * INNER * wide
    return pl.pallas_call(
        functools.partial(kernel, outer, groups),
        out_shape=jax.ShapeDtypeStruct((2, bands, reach), BF16),
        in_specs=[hbm, hbm] + [pl.BlockSpec(memory_space=pltpu.VMEM)] * 4,
        out_specs=hbm,
        scratch_shapes=[
            pltpu.VMEM((2, height, INNER * wide), BF16),
            pltpu.VMEM((INNER, parts, 2, part, wide), BF16),
            pltpu.VMEM((parts, 2, height, part), F32),
            pltpu.VMEM(piece, F32),
            pltpu.VMEM(piece, F32),
            pltpu.VMEM(piece, BF16),
            pltpu.VMEM(piece, BF16),
            pltpu.VMEM((parts, 2, height, part), BF16),
            pltpu.VMEM((INNER, 2, height, wide), BF16),
            pltpu.VMEM((parts, part, part), F32),
            dma((outer,)), dma((outer,)), dma((parts, 6)), dma((parts, 6)), dma((1 + parts, 2)),
        ] + [dma((parts, outer))] * 8 + [
            dma((INNER, outer)), dma((INNER, outer)), dma((INNER,)),
        ],
        compiler_params=pltpu.CompilerParams(
            collective_id=0, has_side_effects=True, vmem_limit_bytes=32 * 1024 * 1024
        ),
        cost_estimate=pl.CostEstimate(flops=flops, bytes_accessed=4 * bands * reach, transcendentals=0),
    )(orbitals, projectors, rows, *maps)


def count_parts(total_proj, per_atom):
    for parts in (3, 2):
        if total_proj % (parts * per_atom) == 0 and total_proj % (parts * 16) == 0:
            return parts
    return 1


def per_device_kernel(outer, groups, orbitals, projectors, coupling, species, offsets):
    total_proj, _, wide = projectors.shape
    per_atom = coupling.shape[1]
    parts = count_parts(total_proj, per_atom)
    part = total_proj // parts
    rows = coupling_rows(coupling, species, offsets, total_proj)
    rows = jnp.transpose(rows.reshape(per_atom, parts, part), (1, 0, 2))
    maps = [jnp.asarray(m) for m in block_maps(part, per_atom)]
    turned = jnp.transpose(projectors, (1, 0, 2)).reshape(2, parts, part, wide)
    result = fused(outer, groups, parts, jnp.transpose(orbitals, (1, 0, 2)), turned, rows, maps)
    return jnp.transpose(result, (1, 0, 2))


def per_device_plain(orbitals, projectors, coupling, species, offsets):
    total_proj = projectors.shape[0]
    p_real, p_imag = projectors[:, 0, :], projectors[:, 1, :]
    rows = coupling_rows(coupling, species, offsets, total_proj)
    matrix = block_diagonal(rows, *block_maps(total_proj, coupling.shape[1]))
    spread = lax.all_to_all(orbitals, "band", split_axis=2, concat_axis=0, tiled=True)
    o_real, o_imag = spread[:, 0, :], spread[:, 1, :]
    partial_sum = jnp.stack(
        [dot_t(o_real, p_real) + dot_t(o_imag, p_imag), dot_t(o_imag, p_real) - dot_t(o_real, p_imag)], axis=1
    )
    becp = lax.psum_scatter(partial_sum, ("ga", "band"), scatter_dimension=0, tiled=True)
    coupled = jnp.einsum("bcp,pq->bcq", becp, matrix, precision=lax.Precision.HIGHEST).astype(BF16)
    dbecp = lax.all_gather(coupled, ("ga", "band"), axis=0, tiled=True)
    d_real, d_imag = dbecp[:, 0, :], dbecp[:, 1, :]
    result = jnp.stack(
        [dot(d_real, p_real) - dot(d_imag, p_imag), dot(d_real, p_imag) + dot(d_imag, p_real)], axis=1
    ).astype(BF16)
    return lax.all_to_all(result, "band", split_axis=0, concat_axis=2, tiled=True)


def solution(mesh):
    groups, members = mesh.shape["ga"], mesh.shape["band"]
    if groups == 2 and members % INNER == 0:
        body = functools.partial(per_device_kernel, members // INNER, groups)
    else:
        body = per_device_plain
    placed = (P("band", None, "ga"), P(None, None, ("ga", "band")), P(), P(), P())
    return jax.shard_map(body, mesh=mesh, in_specs=placed, out_specs=P("band", None, "ga"), check_vma=False)
```

profile of v0, /device:TPU:1, one launch (start us, length us, event | category | flops | bytes accessed | tf_op | source)
XLA Modules:
  0.0 140.8 jit_solution(79314996359445342)
XLA Ops:
  0.0 0.8 select_reduce_fusion
  0.8 0.0 copy-start.3
  0.8 1.0 copy.19
  1.8 0.1 reshape.29
  1.9 0.2 convolution_bitcast_fusion
  2.1 0.1 reshape.30
  2.3 1.8 %copy.18 = bf16[2,864,512]{2,1,0:T(8,128)(2,1)S(1)} copy(bf16[2,864,512]{2,0,1:T(2,128)(2,1)} %bitcast.17) | data formatting | bytes 3538944 | tf_op jit(solution)/shard_map/transpose | solution.py:304
  4.0 0.0 copy-done.3
  4.0 0.0 copy-start
  4.1 0.0 copy-start.1
  4.1 0.0 copy-start.2
  4.1 1.2 copy.24
  5.2 0.0 copy-done
  5.3 0.0 copy-done.1
  5.3 0.0 copy-done.2
  5.3 132.1 %shard_map.82 = bf16[2,64,8192]{2,1,0:T(8,128)(2,1)S(1)} custom-call(bf16[2,64,8192]{2,1,0:T(8,128)(2,1)S(1)} %bitcast.14, bf16[2,3,288,512]{3,2,1,0:T(8,128)(2,1)S(1)} %bitcast.15, f32[3,18,288]{2,1,0:T(8,128)S(1)} %bitcast.16, f32[288,18]{1,0:T(8,128)S(1)} %copy-done.1, s32[288,1]{1,0:T(8,128)S(1)} %copy-done, s32[1,288]{1,0:T(1,128)S(1)} %copy-done.2), custom_call_target="tpu_custom_call" | custom-call | flops 7247757312 | bytes 2097152 | tf_op jit(solution)/shard_map/pallas_call | solution.py:262
  137.4 3.5 %copy.21 = bf16[64,2,8192]{2,1,0:T(2,128)(2,1)} copy(bf16[64,2,8192]{2,0,1:T(8,128)(2,1)S(1)} %bitcast.13) | data formatting | bytes 4194304 | tf_op jit(solution)/shard_map/transpose | solution.py:306
  (3 shorter events, 0.0 us)
Async XLA Ops:
  0.8 3.3 %copy-start.3 = (bf16[64,2,8192]{2,1,0:T(2,128)(2,1)S(1)}, bf16[64,2,8192]{2,1,0:T(2,128)(2,1)}, u32[]{:S(2)}) copy-start(bf16[64,2,8192]{2,1,0:T(2,128)(2,1)} %param.8) | copy-start | bytes 6291460
  4.0 1.2 copy-start
  4.1 1.2 copy-start.1
  4.1 1.2 copy-start.2
where the time goes:
time: 144 us; the launch traced here: 141 us
  Pallas kernels  132 us (92%)
  local copies, waits for them, and re-layouts  7.67 us (5%)
    pallas_call x1, Pallas kernels, fused(): pl.pallas_call(functools.partial(kernel, outer, groups), out_shape=jax.Sh...  132 us
    transpose x1, local copies, waits for them, and re-layouts, per_device_kernel(): return jnp.transpose(result, (1, 0, 2))  3.49 us

commit v1 on v0

v1 whole, which is shorter than its diff:
```python
import functools

import jax
import jax.numpy as jnp
import numpy as np
from jax import lax
from jax.experimental import pallas as pl
from jax.experimental.pallas import tpu as pltpu
from jax.sharding import PartitionSpec as P

MESH = pl.DeviceIdType.MESH
PLANE = 4
LINE = 4
TILE = 8
LANES = 128
F32 = jnp.float32
BF16 = jnp.bfloat16


def coupling_rows(coupling, species, offsets, total_proj):
    kinds, per_atom = coupling.shape[0], coupling.shape[1]
    column = jnp.arange(total_proj, dtype=jnp.int32)
    within = column % per_atom
    start = column - within
    kind = jnp.sum(
        jnp.where(offsets[:, None] == start[None, :], species[:, None], 0), axis=0
    )
    pick = (jnp.arange(kinds * per_atom, dtype=jnp.int32)[:, None] == (kind * per_atom + within)[None, :])
    table = jnp.transpose(coupling, (2, 0, 1)).reshape(per_atom, kinds * per_atom)
    return jnp.dot(table, pick.astype(F32), precision=lax.Precision.HIGHEST, preferred_element_type=F32)


def block_diagonal(rows, spread, start_col, start_row):
    full = lax.dot_general(
        spread, rows, (((1,), (0,)), ((), ())), precision=lax.Precision.HIGHEST, preferred_element_type=F32
    )
    return jnp.where(start_col == start_row, full, 0.0)


def block_maps(count, per_atom):
    index = np.arange(count)
    spread = (index[:, None] % per_atom == np.arange(per_atom)[None, :]).astype(np.float32)
    start = (index // per_atom).astype(np.int32)
    return spread, start[:, None], start[None, :]


def dot_t(a, b):
    return lax.dot_general(a, b, (((1,), (1,)), ((), ())), preferred_element_type=F32)


def dot(a, b):
    return lax.dot_general(a, b, (((1,), (0,)), ((), ())), preferred_element_type=F32)


def flip(bit, by):
    return bit + by - 2 * bit * by


def kernel(
    chunks, o_ref, p_ref, coupling_ref, species_ref, offsets_ref, out_ref,
    obuf, pbuf, coef, zbuf, psend, precv, total, zsend, zrecv, hsum, hsend, hrecv, dbuf, rbuf,
    f_send, f_recv, l_sem, t_send, t_recv, p_send, p_recv, z_send, z_recv, h_send, h_recv,
    e_send, e_recv, d_send, d_recv, r_send, r_recv,
):
    g = lax.axis_index("ga")
    me = lax.axis_index("band")
    proj, wide = p_ref.shape[1], p_ref.shape[2]
    height, width = zbuf.shape[1], zbuf.shape[2]
    unit = 2 * TILE
    members = height // unit
    quarter = height // PLANE
    half = quarter // 2
    per_atom = coupling_ref.shape[1]
    n, z = me % PLANE, me // PLANE
    x, y, z0, z1 = n % 2, n // 2, z % 2, z // 2

    def place(bx, by, b0, b1):
        return (b1 * 2 + b0) * PLANE + by * 2 + bx

    def slot(bx, by, b0, b1):
        return (by * 2 + bx) * LINE + b0 * 2 + b1

    def at(mask):
        bits = (flip(x, mask % 2), flip(y, (mask // 2) % 2), flip(z0, (mask // 4) % 2), flip(z1, mask // 8))
        return place(*bits), slot(*bits)

    my_slot = slot(x, y, z0, z1)
    twin = {"ga": 1 - g}
    plane = [(flip(x, j % 2), flip(y, j // 2)) for j in range(1, PLANE)]
    plane_at = [{"band": place(bx, by, z0, z1)} for bx, by in plane]
    near = {"band": place(x, y, 1 - z0, z1)}
    far = {"band": place(x, y, z0, 1 - z1)}

    def remote(src, dst, send, recv, to):
        return pltpu.make_async_remote_copy(
            src_ref=src, dst_ref=dst, send_sem=send, recv_sem=recv, device_id=to, device_id_type=MESH
        )

    barrier = pltpu.get_barrier_semaphore()
    pl.semaphore_signal(barrier, inc=1, device_id=twin, device_id_type=MESH)

    def greet(mask, carry):
        peer, _ = at(mask)
        for core in range(2):
            pl.semaphore_signal(barrier, inc=1, device_id={"ga": core, "band": peer}, device_id_type=MESH)
        return carry

    lax.fori_loop(1, members, greet, 0)

    def rows_of(i, core):
        return pl.ds(pl.multiple_of((i * 2 + core) * unit, unit), unit)

    def cols_of(index):
        return pl.ds(pl.multiple_of(index * wide, wide), wide)

    my_rows = pl.ds(pl.multiple_of(my_slot * unit, unit), unit)
    my_cols = cols_of(g)

    own_p = pltpu.make_async_copy(p_ref, pbuf.at[:, pl.ds(0, proj), my_cols], l_sem)
    own_p.start()
    for i in range(chunks):
        pltpu.make_async_copy(o_ref.at[rows_of(i, g), cols_of(me)], obuf.at[i, my_rows, my_cols], f_recv.at[i]).start()

    pl.semaphore_wait(barrier, 2 * members - 1)

    twin_p = remote(p_ref, pbuf.at[:, pl.ds(0, proj), my_cols], t_send, t_recv, twin)

    def f_copy(i, core, peer, to):
        return remote(
            o_ref.at[rows_of(i, core), cols_of(peer)], obuf.at[i, my_rows, my_cols], f_send.at[i], f_recv.at[i], to
        )

    def f_issue(i, first, last):
        def step(mask, carry):
            peer, _ = at(mask)
            for core in range(2):
                f_copy(i, core, peer, {"ga": core, "band": peer}).start()
            return carry

        lax.fori_loop(first, last, step, 0)

    def f_twin(i):
        f_copy(i, 1 - g, me, twin).start()

    def whole(ref, send, recv):
        return remote(ref, ref, send, recv, twin)

    def prepare():
        if width > proj:
            for c in range(2):
                pbuf[c, pl.ds(proj, width - proj), :] = jnp.zeros((width - proj, 2 * wide), BF16)
        column = lax.broadcasted_iota(jnp.int32, (offsets_ref.shape[0], width), 1)
        begin = offsets_ref[...]
        inside = (column >= begin) & (column < begin + per_atom)
        kind = jnp.sum(jnp.where(inside, species_ref[...], 0), axis=0, keepdims=True)
        start = jnp.sum(jnp.where(inside, begin, 0), axis=0, keepdims=True)
        within = lax.broadcasted_iota(jnp.int32, (1, width), 1) - start
        index = lax.broadcasted_iota(jnp.int32, (per_atom, width), 0)
        rows = jnp.zeros((per_atom, width), F32)
        for k in range(coupling_ref.shape[0]):
            pick = jnp.where((kind == k) & (within == index), 1.0, 0.0).astype(F32)
            rows = rows + lax.dot_general(
                coupling_ref[k], pick, (((0,), (0,)), ((), ())),
                precision=lax.Precision.HIGHEST, preferred_element_type=F32,
            )
        for s in range(1 - per_atom, per_atom):
            coef[pl.ds(s + per_atom - 1, 1), :] = jnp.sum(
                jnp.where(index == within - s, rows, 0.0), axis=0, keepdims=True
            )

    def piece(index, rows):
        return pl.ds(pl.multiple_of(index * rows, rows), rows)

    def blocks(count):
        step = 2 * LANES
        return [(low, min(step, count - low)) for low in range(0, count, step)]

    def split(value):
        return value.reshape(members, 2, TILE, value.shape[-1])

    def join(real, imag):
        return jnp.stack([real, imag], axis=1).reshape(height, real.shape[-1])

    pcopy, zcopy, hcopy, ecopy, dcopy = {}, {}, {}, {}, {}

    def project(i):
        whole(obuf.at[i], f_send.at[i], f_recv.at[i]).wait_recv()
        for low, size in blocks(width):
            a = split(dot_t(obuf[i], pbuf[0, pl.ds(low, size), :]))
            b = split(dot_t(obuf[i], pbuf[1, pl.ds(low, size), :]))
            zbuf[i, :, pl.ds(low, size)] = join(a[:, 0] + b[:, 1], a[:, 1] - b[:, 0])
        for j in range(PLANE - 1):
            bx, by = plane[j]
            psend[i, j] = zbuf[i, piece(by * 2 + bx, quarter), :].astype(BF16)
            pcopy[i, j] = remote(psend.at[i, j], precv.at[i, j], p_send.at[i, j], p_recv.at[i, j], plane_at[j])
            pcopy[i, j].start()

    def reduce_plane(i):
        value = zbuf[i, piece(n, quarter), :]
        for j in range(PLANE - 1):
            pcopy[i, j].wait_recv()
            value = value + precv[i, j].astype(F32)
        total[i] = value
        zsend[i] = total[i, piece(1 - z0, half), :].astype(BF16)
        zcopy[i] = remote(zsend.at[i], zrecv.at[i], z_send.at[i], z_recv.at[i], near)
        zcopy[i].start()

    def reduce_near(i):
        zcopy[i].wait_recv()
        value = total[i, piece(z0, half), :] + zrecv[i].astype(F32)
        hsum[i] = value
        hsend[i] = value.astype(BF16)
        hcopy[i] = remote(hsend.at[i], hrecv.at[i], h_send.at[i], h_recv.at[i], far)
        hcopy[i].start()

    def couple(i):
        hcopy[i].wait_recv()
        value = hsum[i] + hrecv[i].astype(F32)
        result = jnp.zeros_like(value)
        for s in range(1 - per_atom, per_atom):
            moved = value if s == 0 else pltpu.roll(value, s % width, 1)
            result = result + moved * coef[pl.ds(s + per_atom - 1, 1), :]
        mine = piece(n * 2 + z0, half)
        dbuf[i, mine, :] = result.astype(BF16)
        own = dbuf.at[i, mine, :]
        ecopy[i] = remote(own, own, e_send.at[i], e_recv.at[i], near)
        ecopy[i].start()
        for j in range(PLANE - 1):
            dcopy[i, 0, j] = remote(own, own, d_send.at[i, 0, j], d_recv.at[i, 0, j], plane_at[j])
            dcopy[i, 0, j].start()

    def hand_on(i):
        ecopy[i].wait_recv()
        got = dbuf.at[i, piece(n * 2 + 1 - z0, half), :]
        for j in range(PLANE - 1):
            dcopy[i, 1, j] = remote(got, got, d_send.at[i, 1, j], d_recv.at[i, 1, j], plane_at[j])
            dcopy[i, 1, j].start()

    def r_copy(i, there, core, to):
        rows = pl.ds(pl.multiple_of(there * unit, unit), unit)
        return remote(
            rbuf.at[i, rows, cols_of(core)], out_ref.at[rows_of(i, g), cols_of(me)], r_send.at[i], r_recv.at[i], to
        )

    def apply(i):
        for v in range(2):
            for j in range(PLANE - 1):
                dcopy[i, v, j].wait_recv()
        for low, size in blocks(2 * wide):
            a = split(dot(dbuf[i], pbuf[0, :, pl.ds(low, size)]))
            b = split(dot(dbuf[i], pbuf[1, :, pl.ds(low, size)]))
            rbuf[i, :, pl.ds(low, size)] = join(a[:, 0] - b[:, 1], b[:, 0] + a[:, 1]).astype(BF16)

        def step(mask, carry):
            peer, there = at(mask)
            for core in range(2):
                r_copy(i, there, core, {"ga": core, "band": peer}).start()
            return carry

        lax.fori_loop(1, members, step, 0)
        r_copy(i, my_slot, 1 - g, twin).start()
        pltpu.make_async_copy(
            rbuf.at[i, my_rows, cols_of(g)], out_ref.at[rows_of(i, g), cols_of(me)], r_recv.at[i]
        ).start()

    twin_p.start()
    f_twin(0)
    f_issue(0, 1, members)
    f_twin(1)
    f_issue(1, 1, members)
    prepare()
    own_p.wait()
    twin_p.wait_recv()

    for i in range(2, chunks):
        f_twin(i)
    project(0)
    f_issue(2, 1, members)
    reduce_plane(0)
    reduce_near(0)
    project(1)
    f_issue(3, 1, members)
    couple(0)
    reduce_plane(1)
    hand_on(0)
    reduce_near(1)
    project(2)
    apply(0)
    couple(1)
    reduce_plane(2)
    hand_on(1)
    reduce_near(2)
    project(3)
    apply(1)
    couple(2)
    reduce_plane(3)
    hand_on(2)
    reduce_near(3)
    apply(2)
    couple(3)
    hand_on(3)
    apply(3)

    twin_p.wait_send()
    for copies in (pcopy, zcopy, hcopy, ecopy, dcopy):
        for copy in copies.values():
            copy.wait_send()
    sent = pl.ds(0, height - unit // 2)
    for i in range(chunks):
        whole(obuf.at[i, sent, :], f_send.at[i], f_recv.at[i]).wait_send()
        whole(rbuf.at[i, sent, :], r_send.at[i], r_recv.at[i]).wait_send()
        whole(out_ref.at[pl.ds(i * 2 * unit, 2 * unit), :], r_send.at[i], r_recv.at[i]).wait_recv()


def fused(chunks, members, orbitals, projectors, coupling, species, offsets):
    rows, reach = orbitals.shape
    _, proj, wide = projectors.shape
    width = -(-proj // LANES) * LANES
    height = members * 2 * TILE
    quarter = height // PLANE
    half = quarter // 2
    per_atom = coupling.shape[1]
    taps = -(-(2 * per_atom - 1) // TILE) * TILE + TILE
    dma = pltpu.SemaphoreType.DMA
    hbm = pl.BlockSpec(memory_space=pl.ANY)
    flops = 32 * chunks * height * width * wide
    vm = pltpu.VMEM
    return pl.pallas_call(
        functools.partial(kernel, chunks),
        out_shape=jax.ShapeDtypeStruct((rows, reach), BF16),
        in_specs=[hbm, hbm] + [pl.BlockSpec(memory_space=pltpu.VMEM)] * 3,
        out_specs=hbm,
        scratch_shapes=[
            vm((chunks, height, 2 * wide), BF16),
            vm((2, width, 2 * wide), BF16),
            vm((taps, width), F32),
            vm((chunks, height, width), F32),
            vm((chunks, PLANE - 1, quarter, width), BF16),
            vm((chunks, PLANE - 1, quarter, width), BF16),
            vm((chunks, quarter, width), F32),
            vm((chunks, half, width), BF16),
            vm((chunks, half, width), BF16),
            vm((chunks, half, width), F32),
            vm((chunks, half, width), BF16),
            vm((chunks, half, width), BF16),
            vm((chunks, height, width), BF16),
            vm((chunks, height, 2 * wide), BF16),
            dma((chunks,)), dma((chunks,)), dma, dma, dma,
            dma((chunks, PLANE - 1)), dma((chunks, PLANE - 1)),
            dma((chunks,)), dma((chunks,)), dma((chunks,)), dma((chunks,)), dma((chunks,)), dma((chunks,)),
            dma((chunks, 2, PLANE - 1)), dma((chunks, 2, PLANE - 1)),
            dma((chunks,)), dma((chunks,)),
        ],
        compiler_params=pltpu.CompilerParams(
            collective_id=0, has_side_effects=True, vmem_limit_bytes=48 * 1024 * 1024
        ),
        cost_estimate=pl.CostEstimate(flops=flops, bytes_accessed=4 * rows * reach, transcendentals=0),
    )(orbitals, projectors, coupling, species, offsets)


def per_device_kernel(groups, members, orbitals, projectors, coupling, species, offsets):
    bands, _, reach = orbitals.shape
    blocks = bands // TILE
    turned = jnp.transpose(orbitals.reshape(blocks, TILE, 2, reach), (0, 2, 1, 3)).reshape(2 * bands, reach)
    result = fused(
        blocks // groups, members, turned, jnp.transpose(projectors, (1, 0, 2)), coupling,
        species[:, None], offsets[:, None],
    )
    return jnp.transpose(result.reshape(blocks, 2, TILE, reach), (0, 2, 1, 3)).reshape(bands, 2, reach)


def per_device_plain(orbitals, projectors, coupling, species, offsets):
    total_proj = projectors.shape[0]
    p_real, p_imag = projectors[:, 0, :], projectors[:, 1, :]
    rows = coupling_rows(coupling, species, offsets, total_proj)
    matrix = block_diagonal(rows, *block_maps(total_proj, coupling.shape[1]))
    spread = lax.all_to_all(orbitals, "band", split_axis=2, concat_axis=0, tiled=True)
    o_real, o_imag = spread[:, 0, :], spread[:, 1, :]
    partial_sum = jnp.stack(
        [dot_t(o_real, p_real) + dot_t(o_imag, p_imag), dot_t(o_imag, p_real) - dot_t(o_real, p_imag)], axis=1
    )
    becp = lax.psum_scatter(partial_sum, ("ga", "band"), scatter_dimension=0, tiled=True)
    coupled = jnp.einsum("bcp,pq->bcq", becp, matrix, precision=lax.Precision.HIGHEST).astype(BF16)
    dbecp = lax.all_gather(coupled, ("ga", "band"), axis=0, tiled=True)
    d_real, d_imag = dbecp[:, 0, :], dbecp[:, 1, :]
    result = jnp.stack(
        [dot(d_real, p_real) - dot(d_imag, p_imag), dot(d_real, p_imag) + dot(d_imag, p_real)], axis=1
    ).astype(BF16)
    return lax.all_to_all(result, "band", split_axis=0, concat_axis=2, tiled=True)


def solution(mesh):
    groups, members = mesh.shape["ga"], mesh.shape["band"]

    def body(orbitals, projectors, *rest):
        if groups == 2 and members == PLANE * LINE and orbitals.shape[0] == 4 * groups * TILE:
            return per_device_kernel(groups, members, orbitals, projectors, *rest)
        return per_device_plain(orbitals, projectors, *rest)

    placed = (P("band", None, "ga"), P(None, None, ("ga", "band")), P(), P(), P())
    return jax.shard_map(body, mesh=mesh, in_specs=placed, out_specs=P("band", None, "ga"), check_vma=False)
```

time: 144 us -> 128 us (0.89); the launches traced: 141 us -> 127 us
  Pallas kernels: 132 us -> 118 us
    pallas_call x1, Pallas kernels: 132 us -> 118 us  [fused(): pl.pallas_call(functools.partial(kernel, chunks), out_shape=jax.ShapeDtyp...]
    transpose x3 -> x1, local copies, waits for them, and re-layouts: 6.28 us -> 3.5 us  [per_device_kernel(): jnp.transpose(result.reshape(blocks, 2, TILE, reach), (0, 2, 1, 3))]
    broadcast_in_dim x0 -> x2, local copies, waits for them, and re-layouts: none -> 1.63 us  [the longest x1 0.89 us: per_device_kernel(): species[:, None]]
where the time goes in v1:
time: 128 us; the launch traced here: 127 us
  Pallas kernels  118 us (92%)
  local copies, waits for them, and re-layouts  8.83 us (7%)
    pallas_call x1, Pallas kernels, fused(): pl.pallas_call(functools.partial(kernel, chunks), out_shape=jax.ShapeDtyp...  118 us
    transpose x1, local copies, waits for them, and re-layouts, per_device_kernel(): jnp.transpose(result.reshape(blocks, 2, TILE, reach), (0, 2, 1, 3))  3.5 us

profile of v1, /device:TPU:1, one launch (start us, length us, event | category | flops | bytes accessed | tf_op | source)
XLA Modules:
  0.0 127.0 jit_solution(15855832200815691992)
XLA Ops:
  0.0 0.0 copy-start
  0.0 0.9 copy.9.species_ref
  0.9 0.7 copy.10.offsets_ref
  1.6 0.8 copy.8.coupling_ref
  2.4 1.8 %copy.13 = bf16[864,2,512]{2,0,1:T(8,128)(2,1)S(1)} copy(bf16[864,2,512]{2,1,0:T(2,128)(2,1)} %param.6) | data formatting | bytes 3538944 | tf_op args[1]
  4.2 0.0 copy-done
  4.2 1.2 copy.6
  5.3 118.1 %shard_map.55 = bf16[128,8192]{1,0:T(8,128)(2,1)S(1)} custom-call(bf16[128,8192]{1,0:T(8,128)(2,1)S(1)} %bitcast.14, bf16[2,864,512]{2,1,0:T(8,128)(2,1)S(1)} %bitcast.15, f32[4,18,18]{2,1,0:T(8,128)S(1)} %copy.8.coupling_ref, s32[48,1]{1,0:T(8,128)S(1)} %copy.9.species_ref, s32[48,1]{1,0:T(8,128)S(1)} %copy.10.offsets_ref), custom_call_target="tpu_custom_call" | custom-call | flops 15032385536 | bytes 4194304 | tf_op jit(solution)/shard_map/pallas_call | solution.py:328
  123.5 3.5 %copy.11 = bf16[8,8,2,8192]{3,2,1,0:T(2,128)(2,1)} copy(bf16[8,8,2,8192]{3,1,2,0:T(8,128)(2,1)S(1)} %bitcast.13) | data formatting | bytes 4194304 | tf_op jit(solution)/shard_map/transpose | solution.py:369
Async XLA Ops:
  0.0 4.2 %copy-start = (bf16[64,2,8192]{2,1,0:T(2,128)(2,1)S(1)}, bf16[64,2,8192]{2,1,0:T(2,128)(2,1)}, u32[]{:S(2)}) copy-start(bf16[64,2,8192]{2,1,0:T(2,128)(2,1)} %param.5) | copy-start | bytes 6291460

commit v2 on v1

v2 whole, which is shorter than its diff:
```python
import functools

import jax
import jax.numpy as jnp
import numpy as np
from jax import lax
from jax.experimental import pallas as pl
from jax.experimental.pallas import tpu as pltpu
from jax.sharding import PartitionSpec as P

MESH = pl.DeviceIdType.MESH
PLANE = 4
LINE = 4
TILE = 8
LANES = 128
F32 = jnp.float32
BF16 = jnp.bfloat16
VMEM_LIMIT = 63 * 1024 * 1024
WINDOW = 16
DELAYS = (12, 16, 20, 24, 28)


def coupling_rows(coupling, species, offsets, total_proj):
    kinds, per_atom = coupling.shape[0], coupling.shape[1]
    column = jnp.arange(total_proj, dtype=jnp.int32)
    within = column % per_atom
    start = column - within
    kind = jnp.sum(
        jnp.where(offsets[:, None] == start[None, :], species[:, None], 0), axis=0
    )
    pick = (jnp.arange(kinds * per_atom, dtype=jnp.int32)[:, None] == (kind * per_atom + within)[None, :])
    table = jnp.transpose(coupling, (2, 0, 1)).reshape(per_atom, kinds * per_atom)
    return jnp.dot(table, pick.astype(F32), precision=lax.Precision.HIGHEST, preferred_element_type=F32)


def block_diagonal(rows, spread, start_col, start_row):
    full = lax.dot_general(
        spread, rows, (((1,), (0,)), ((), ())), precision=lax.Precision.HIGHEST, preferred_element_type=F32
    )
    return jnp.where(start_col == start_row, full, 0.0)


def block_maps(count, per_atom):
    index = np.arange(count)
    spread = (index[:, None] % per_atom == np.arange(per_atom)[None, :]).astype(np.float32)
    start = (index // per_atom).astype(np.int32)
    return spread, start[:, None], start[None, :]


def dot_t(a, b):
    return lax.dot_general(a, b, (((1,), (1,)), ((), ())), preferred_element_type=F32)


def dot(a, b):
    return lax.dot_general(a, b, (((1,), (0,)), ((), ())), preferred_element_type=F32)


def flip(bit, by):
    return bit + by - 2 * bit * by


def kernel(
    chunks, o_ref, p_ref, coupling_ref, species_ref, offsets_ref, out_ref,
    obuf, praw, table, atoms, lbuf, pbuf, coef, zbuf, psend, precv, total, zsend, zrecv, hsum, hsend, hrecv, dbuf, rbuf,
    f_send, f_recv, l_sem, t_send, t_recv, p_send, p_recv, z_send, z_recv, h_send, h_recv,
    e_send, e_recv, d_send, d_recv, r_send, r_recv,
):
    g = lax.axis_index("ga")
    me = lax.axis_index("band")
    proj, wide = p_ref.shape[0], p_ref.shape[2]
    height, width = zbuf.shape[2], zbuf.shape[3]
    members = height // TILE
    quarter = height // PLANE
    half = quarter // 2
    per_atom = coupling_ref.shape[0]
    n, z = me % PLANE, me // PLANE
    x, y, z0, z1 = n % 2, n // 2, z % 2, z // 2

    def place(bx, by, b0, b1):
        return (b1 * 2 + b0) * PLANE + by * 2 + bx

    def slot(bx, by, b0, b1):
        return (by * 2 + bx) * LINE + b0 * 2 + b1

    def at(mask):
        bits = (flip(x, mask % 2), flip(y, (mask // 2) % 2), flip(z0, (mask // 4) % 2), flip(z1, mask // 8))
        return place(*bits), slot(*bits)

    my_slot = slot(x, y, z0, z1)
    twin = {"ga": 1 - g}
    plane = [(flip(x, j % 2), flip(y, j // 2)) for j in range(1, PLANE)]
    plane_at = [{"band": place(bx, by, z0, z1)} for bx, by in plane]
    near = {"band": place(x, y, 1 - z0, z1)}
    far = {"band": place(x, y, z0, 1 - z1)}
    peers = [None] + [at(mask) for mask in range(1, members)]

    def remote(src, dst, send, recv, to):
        return pltpu.make_async_remote_copy(
            src_ref=src, dst_ref=dst, send_sem=send, recv_sem=recv, device_id=to, device_id_type=MESH
        )

    barrier = pltpu.get_barrier_semaphore()
    pl.semaphore_signal(barrier, inc=1, device_id=twin, device_id_type=MESH)
    for mask in range(1, members):
        for core in range(2):
            pl.semaphore_signal(
                barrier, inc=1, device_id={"ga": core, "band": peers[mask][0]}, device_id_type=MESH
            )

    def piece(index, rows):
        return pl.ds(pl.multiple_of(index * rows, rows), rows)

    def rows_of(i, core):
        return piece(i * 2 + core, TILE)

    def cols_of(index):
        return piece(index, wide)

    my_rows = piece(my_slot, TILE)
    my_cols = cols_of(g)

    local = [
        pltpu.make_async_copy(p_ref, praw.at[g], l_sem.at[0]),
        pltpu.make_async_copy(coupling_ref, table, l_sem.at[1]),
        pltpu.make_async_copy(species_ref, atoms.at[0], l_sem.at[2]),
        pltpu.make_async_copy(offsets_ref, atoms.at[1], l_sem.at[3]),
    ]
    for copy in local:
        copy.start()
    for i in range(chunks):
        pltpu.make_async_copy(
            o_ref.at[rows_of(i, g), :, cols_of(me)], obuf.at[i, my_rows, :, my_cols], f_recv.at[i]
        ).start()

    pl.semaphore_wait(barrier, 2 * members - 1)

    twin_p = remote(p_ref, praw.at[g], t_send, t_recv, twin)

    def f_copy(i, q, core, peer, to, block=None):
        rows = rows_of(i, core if block is None else block)
        return remote(
            o_ref.at[rows, :, cols_of(peer)], obuf.at[i, my_rows, :, my_cols],
            f_send.at[i, q, core], f_recv.at[i], to,
        )

    def batch(q):
        inside = [q + 1] if q + 1 < PLANE else []
        return inside + [step * PLANE + q for step in range(1, members // PLANE)]

    def f_part(i, q, core):
        for mask in batch(q):
            peer, _ = peers[mask]
            f_copy(i, q, core, peer, {"ga": core, "band": peer}).start()

    def f_twin(i):
        f_copy(i, PLANE, 0, me, twin, 1 - g).start()

    def whole(ref, send, recv):
        return remote(ref, ref, send, recv, twin)

    def prepare():
        for copy in local:
            copy.wait()
        count = atoms.shape[2]
        turn = lax.broadcasted_iota(jnp.int32, (count, count), 0) == lax.broadcasted_iota(jnp.int32, (count, count), 1)

        def upright(row):
            return jnp.sum(jnp.where(turn, row.astype(F32), 0.0), axis=1, keepdims=True)

        column = lax.broadcasted_iota(jnp.int32, (count, width), 1).astype(F32)
        begin = upright(atoms[1])
        inside = (column >= begin) & (column < begin + per_atom)
        kind = jnp.sum(jnp.where(inside, upright(atoms[0]), 0.0), axis=0, keepdims=True)
        start = jnp.sum(jnp.where(inside, begin, 0.0), axis=0, keepdims=True)
        kind = (kind + 0.5).astype(jnp.int32)
        within = lax.broadcasted_iota(jnp.int32, (1, width), 1) - (start + 0.5).astype(jnp.int32)
        index = lax.broadcasted_iota(jnp.int32, (per_atom, width), 0)
        rows = jnp.zeros((per_atom, width), F32)
        for k in range(coupling_ref.shape[1]):
            pick = jnp.where((kind == k) & (within == index), 1.0, 0.0).astype(F32)
            rows = rows + lax.dot_general(
                table[:, k, :], pick, (((0,), (0,)), ((), ())),
                precision=lax.Precision.HIGHEST, preferred_element_type=F32,
            )
        for s in range(1 - per_atom, per_atom):
            coef[pl.ds(s + per_atom - 1, 1), :] = jnp.sum(
                jnp.where(index == within - s, rows, 0.0), axis=0, keepdims=True
            )
        twin_p.wait_recv()
        for c in range(2):
            for core in range(2):
                cols = pl.ds(core * wide, wide)
                if width > proj:
                    pbuf[c, pl.ds(proj, width - proj), cols] = jnp.zeros((width - proj, wide), BF16)

        def unpack(r, carry):
            rows = piece(r, 2 * TILE)
            for core in range(2):
                pbuf[:, rows, pl.ds(core * wide, wide)] = jnp.swapaxes(praw[core, rows], 0, 1)
            return carry

        lax.fori_loop(0, proj // (2 * TILE), unpack, 0)

    def blocks(count):
        step = 2 * LANES
        return [(low, min(step, count - low)) for low in range(0, count, step)]

    pcopy, zcopy, hcopy, ecopy, dcopy = {}, {}, {}, {}, {}

    def project(i):
        whole(obuf.at[i], f_send.at[i, 0, 0], f_recv.at[i]).wait_recv()
        for r in range(0, height, 2 * TILE):
            lbuf[:, pl.ds(r, 2 * TILE), :] = jnp.swapaxes(obuf[i, pl.ds(r, 2 * TILE)], 0, 1)
        left = lbuf[...].reshape(2 * height, 2 * wide)
        for low, size in blocks(width):
            a = dot_t(left, pbuf[0, pl.ds(low, size), :])
            b = dot_t(left, pbuf[1, pl.ds(low, size), :])
            zbuf[i, 0, :, pl.ds(low, size)] = a[:height] + b[height:]
            zbuf[i, 1, :, pl.ds(low, size)] = a[height:] - b[:height]
        for j in range(PLANE - 1):
            bx, by = plane[j]
            psend[i, j] = zbuf[i, :, piece(by * 2 + bx, quarter), :].astype(BF16)
            pcopy[i, j] = remote(psend.at[i, j], precv.at[i, j], p_send.at[i, j], p_recv.at[i, j], plane_at[j])
            pcopy[i, j].start()

    def reduce_plane(i):
        value = zbuf[i, :, piece(n, quarter), :]
        for j in range(PLANE - 1):
            pcopy[i, j].wait_recv()
            value = value + precv[i, j].astype(F32)
        total[i] = value
        zsend[i] = total[i, :, piece(1 - z0, half), :].astype(BF16)
        zcopy[i] = remote(zsend.at[i], zrecv.at[i], z_send.at[i], z_recv.at[i], near)
        zcopy[i].start()

    def reduce_near(i):
        zcopy[i].wait_recv()
        value = total[i, :, piece(z0, half), :] + zrecv[i].astype(F32)
        hsum[i] = value
        hsend[i] = value.astype(BF16)
        hcopy[i] = remote(hsend.at[i], hrecv.at[i], h_send.at[i], h_recv.at[i], far)
        hcopy[i].start()

    def couple(i):
        hcopy[i].wait_recv()
        value = (hsum[i] + hrecv[i].astype(F32)).reshape(2 * half, width)
        result = jnp.zeros_like(value)
        for s in range(1 - per_atom, per_atom):
            moved = value if s == 0 else pltpu.roll(value, s % width, 1)
            result = result + moved * coef[pl.ds(s + per_atom - 1, 1), :]
        mine = piece(n * 2 + z0, half)
        dbuf[i, :, mine, :] = result.astype(BF16).reshape(2, half, width)
        own = dbuf.at[i, :, mine, :]
        ecopy[i] = remote(own, own, e_send.at[i], e_recv.at[i], near)
        ecopy[i].start()
        for j in range(PLANE - 1):
            dcopy[i, 0, j] = remote(own, own, d_send.at[i, 0, j], d_recv.at[i, 0, j], plane_at[j])
            dcopy[i, 0, j].start()

    def hand_on(i):
        ecopy[i].wait_recv()
        got = dbuf.at[i, :, piece(n * 2 + 1 - z0, half), :]
        for j in range(PLANE - 1):
            dcopy[i, 1, j] = remote(got, got, d_send.at[i, 1, j], d_recv.at[i, 1, j], plane_at[j])
            dcopy[i, 1, j].start()

    def r_copy(i, q, core, there, to, block=None):
        return remote(
            rbuf.at[i, piece(there, TILE), :, cols_of(core if block is None else block)],
            out_ref.at[rows_of(i, g), :, cols_of(me)], r_send.at[i, q, core], r_recv.at[i], to,
        )

    def r_part(i, q, core):
        for mask in batch(q):
            peer, there = peers[mask]
            r_copy(i, q, core, there, {"ga": core, "band": peer}).start()

    def sent(k):
        phase, i, q, core = batches[k]
        ref = (obuf, rbuf)[phase].at[i, pl.ds(0, len(batch(q)) * TILE // 2)]
        send = (f_send, r_send)[phase].at[i, q, core]
        whole(ref, send, (f_recv, r_recv)[phase].at[i]).wait_send()

    def apply(i, core):
        if core == 0:
            for v in range(2):
                for j in range(PLANE - 1):
                    dcopy[i, v, j].wait_recv()
        left = dbuf[i].reshape(2 * height, width)
        for low, size in blocks(wide):
            cols = pl.ds(core * wide + low, size)
            a = dot(left, pbuf[0, :, cols])
            b = dot(left, pbuf[1, :, cols])
            both = jnp.stack([a[:height] - b[height:], b[:height] + a[height:]]).astype(BF16)
            for r in range(0, height, 2 * TILE):
                rbuf[i, pl.ds(r, 2 * TILE), :, cols] = jnp.swapaxes(both[:, r : r + 2 * TILE], 0, 1)
        if core == 1:
            r_copy(i, PLANE, 0, my_slot, twin, 1 - g).start()
            pltpu.make_async_copy(
                rbuf.at[i, my_rows, :, cols_of(g)], out_ref.at[rows_of(i, g), :, cols_of(me)], r_recv.at[i]
            ).start()

    batches = [
        (phase, i, q, core)
        for phase in range(2) for i in range(chunks) for core in range(2) for q in range(PLANE)
    ]
    each = 2 * PLANE
    stages = (project, reduce_plane, reduce_near, couple, hand_on)
    plan = {}
    for i in range(chunks):
        for stage, delay in zip(stages, DELAYS):
            plan.setdefault(min(i * each + delay, len(batches) // 2 + i * each), []).append((stage, i))

    twin_p.start()
    for k, (phase, i, q, core) in enumerate(batches):
        for stage, index in sorted(plan.get(k, []), key=lambda item: item[1]):
            stage(index)
        if k == each // 2:
            prepare()
        if k >= WINDOW:
            sent(k - WINDOW)
        if phase:
            if q == 0:
                apply(i, core)
            r_part(i, q, core)
        else:
            if core + q == 0:
                f_twin(i)
            f_part(i, q, core)

    for k in range(len(batches) - WINDOW, len(batches)):
        sent(k)
    twin_p.wait_send()
    for copies in (pcopy, zcopy, hcopy, ecopy, dcopy):
        for copy in copies.values():
            copy.wait_send()
    single = pl.ds(0, TILE // 2)
    for i in range(chunks):
        whole(obuf.at[i, single], f_send.at[i, PLANE, 0], f_recv.at[i]).wait_send()
        whole(rbuf.at[i, single], r_send.at[i, PLANE, 0], r_recv.at[i]).wait_send()
        whole(out_ref.at[pl.ds(i * 2 * TILE, 2 * TILE)], r_send.at[i, PLANE, 0], r_recv.at[i]).wait_recv()


def fused(chunks, members, orbitals, projectors, coupling, species, offsets):
    bands, _, reach = orbitals.shape
    proj, _, wide = projectors.shape
    width = -(-proj // LANES) * LANES
    height = members * TILE
    quarter = height // PLANE
    half = quarter // 2
    per_atom = coupling.shape[0]
    taps = -(-(2 * per_atom - 1) // TILE) * TILE + TILE
    dma = pltpu.SemaphoreType.DMA
    hbm = pl.BlockSpec(memory_space=pl.ANY)
    flops = 64 * chunks * height * width * wide
    vm = pltpu.VMEM
    steps = dma((chunks,))
    return pl.pallas_call(
        functools.partial(kernel, chunks),
        out_shape=jax.ShapeDtypeStruct(orbitals.shape, BF16),
        in_specs=[hbm] * 5,
        out_specs=hbm,
        scratch_shapes=[
            vm((chunks, height, 2, 2 * wide), BF16),
            vm((2, proj, 2, wide), BF16),
            vm(coupling.shape, F32),
            vm((2,) + species.shape, jnp.int32),
            vm((2, height, 2 * wide), BF16),
            vm((2, width, 2 * wide), BF16),
            vm((taps, width), F32),
            vm((chunks, 2, height, width), F32),
            vm((chunks, PLANE - 1, 2, quarter, width), BF16),
            vm((chunks, PLANE - 1, 2, quarter, width), BF16),
            vm((chunks, 2, quarter, width), F32),
            vm((chunks, 2, half, width), BF16),
            vm((chunks, 2, half, width), BF16),
            vm((chunks, 2, half, width), F32),
            vm((chunks, 2, half, width), BF16),
            vm((chunks, 2, half, width), BF16),
            vm((chunks, 2, height, width), BF16),
            vm((chunks, height, 2, 2 * wide), BF16),
            dma((chunks, PLANE + 1, 2)), steps, dma((4,)), dma, dma,
            dma((chunks, PLANE - 1)), dma((chunks, PLANE - 1)),
            steps, steps, steps, steps, steps, steps,
            dma((chunks, 2, PLANE - 1)), dma((chunks, 2, PLANE - 1)),
            dma((chunks, PLANE + 1, 2)), steps,
        ],
        compiler_params=pltpu.CompilerParams(
            collective_id=0, has_side_effects=True, vmem_limit_bytes=VMEM_LIMIT
        ),
        cost_estimate=pl.CostEstimate(flops=flops, bytes_accessed=8 * bands * reach, transcendentals=0),
    )(orbitals, projectors, coupling, species, offsets)


def per_device_kernel(groups, members, orbitals, projectors, coupling, species, offsets):
    chunks = orbitals.shape[0] // (groups * TILE)
    return fused(
        chunks, members, orbitals, projectors, jnp.transpose(coupling, (1, 0, 2)), species[None, :], offsets[None, :]
    )


def per_device_plain(orbitals, projectors, coupling, species, offsets):
    total_proj = projectors.shape[0]
    p_real, p_imag = projectors[:, 0, :], projectors[:, 1, :]
    rows = coupling_rows(coupling, species, offsets, total_proj)
    matrix = block_diagonal(rows, *block_maps(total_proj, coupling.shape[1]))
    spread = lax.all_to_all(orbitals, "band", split_axis=2, concat_axis=0, tiled=True)
    o_real, o_imag = spread[:, 0, :], spread[:, 1, :]
    partial_sum = jnp.stack(
        [dot_t(o_real, p_real) + dot_t(o_imag, p_imag), dot_t(o_imag, p_real) - dot_t(o_real, p_imag)], axis=1
    )
    becp = lax.psum_scatter(partial_sum, ("ga", "band"), scatter_dimension=0, tiled=True)
    coupled = jnp.einsum("bcp,pq->bcq", becp, matrix, precision=lax.Precision.HIGHEST).astype(BF16)
    dbecp = lax.all_gather(coupled, ("ga", "band"), axis=0, tiled=True)
    d_real, d_imag = dbecp[:, 0, :], dbecp[:, 1, :]
    result = jnp.stack(
        [dot(d_real, p_real) - dot(d_imag, p_imag), dot(d_real, p_imag) + dot(d_imag, p_real)], axis=1
    ).astype(BF16)
    return lax.all_to_all(result, "band", split_axis=0, concat_axis=2, tiled=True)


def solution(mesh):
    groups, members = mesh.shape["ga"], mesh.shape["band"]

    def body(orbitals, projectors, *rest):
        fits = orbitals.shape[0] % (groups * TILE) == 0 and projectors.shape[0] % (2 * TILE) == 0
        if groups == 2 and members == PLANE * LINE and fits:
            return per_device_kernel(groups, members, orbitals, projectors, *rest)
        return per_device_plain(orbitals, projectors, *rest)

    placed = (P("band", None, "ga"), P(None, None, ("ga", "band")), P(), P(), P())
    return jax.shard_map(body, mesh=mesh, in_specs=placed, out_specs=P("band", None, "ga"), check_vma=False)
```

time: 128 us -> 119 us (0.930)
  Pallas kernels: 118 us -> 113 us
  local copies, waits for them, and re-layouts: 8.83 us -> 6.02 us
    pallas_call x1, Pallas kernels: 118 us -> 113 us  [fused(): pl.pallas_call(functools.partial(kernel, chunks), out_shape=jax.ShapeDtyp...]
    transpose x1 -> x0, local copies, waits for them, and re-layouts: 3.5 us -> none  [per_device_kernel(): jnp.transpose(result.reshape(blocks, 2, TILE, reach), (0, 2, 1, 3))]
    unnamed x4 -> x1, local copies, waits for them, and re-layouts: 2.53 us -> 6.02 us
    broadcast_in_dim x2 -> x0, local copies, waits for them, and re-layouts: 1.63 us -> none  [the longest x1 0.89 us: per_device_kernel(): species[:, None]]
where the time goes in v2:
time: 119 us
  Pallas kernels  113 us (95%)
  local copies, waits for them, and re-layouts  6.02 us (5%)
    pallas_call x1, Pallas kernels, fused(): pl.pallas_call(functools.partial(kernel, chunks), out_shape=jax.ShapeDtyp...  113 us
    unnamed x1, local copies, waits for them, and re-layouts  6.02 us

profile of v2, /device:TPU:1, one launch (start us, length us, event | category | flops | bytes accessed | tf_op | source)
XLA Modules:
  0.0 119.0 jit_solution(8598044639601206470)
XLA Ops:
  0.0 112.9 %shard_map.55 = bf16[64,2,8192]{2,1,0:T(2,128)(2,1)} custom-call(bf16[64,2,8192]{2,1,0:T(2,128)(2,1)} %o_ref.1, bf16[864,2,512]{2,1,0:T(2,128)(2,1)} %p_ref.1, f32[18,4,18]{2,1,0:T(4,128)} %bitcast.3, s32[1,48]{1,0:T(1,128)} %bitcast.4, s32[1,48]{1,0:T(1,128)} %bitcast.5), custom_call_target="tpu_custom_call" | custom-call | flops 15032385536 | bytes 4194304 | tf_op jit(solution)/shard_map/pallas_call | solution.py:358
  113.0 6.0 %copy.7 = bf16[64,2,8192]{2,1,0:T(2,128)(2,1)} copy(bf16[64,2,8192]{2,1,0:T(2,128)(2,1)} %shard_map.55) | data formatting | bytes 4194304

commit v3 on v2

--- a/solution.py
+++ b/solution.py
@@ -16,8 +16,13 @@
 F32 = jnp.float32
 BF16 = jnp.bfloat16
 VMEM_LIMIT = 63 * 1024 * 1024
-WINDOW = 16
-DELAYS = (12, 16, 20, 24, 28)
+WINDOW = 64
+DELAYS = (
+    (12, 16, 20, 24, 28),
+    (12, 16, 20, 24, 28),
+    (12, 16, 20, 24, 28),
+    (12, 17, 20, 24, 28),
+)
 
 
 def coupling_rows(coupling, species, offsets, total_proj):
@@ -308,7 +313,7 @@
     stages = (project, reduce_plane, reduce_near, couple, hand_on)
     plan = {}
     for i in range(chunks):
-        for stage, delay in zip(stages, DELAYS):
+        for stage, delay in zip(stages, DELAYS[min(i, len(DELAYS) - 1)]):
             plan.setdefault(min(i * each + delay, len(batches) // 2 + i * each), []).append((stage, i))
 
     twin_p.start()
@@ -328,7 +333,7 @@
                 f_twin(i)
             f_part(i, q, core)
 
-    for k in range(len(batches) - WINDOW, len(batches)):
+    for k in range(max(len(batches) - WINDOW, 0), len(batches)):
         sent(k)
     twin_p.wait_send()
     for copies in (pcopy, zcopy, hcopy, ecopy, dcopy):
@@ -392,11 +397,43 @@
     )(orbitals, projectors, coupling, species, offsets)
 
 
+def settle_kernel(src_ref, dst_ref, buf, in_sem, out_sem):
+    pieces = in_sem.shape[0]
+    rows = src_ref.shape[0] // pieces
+    pulls, pushes = [], []
+    for i in range(pieces):
+        part = pl.ds(i * rows, rows)
+        pulls.append(pltpu.make_async_copy(src_ref.at[part], buf.at[part], in_sem.at[i]))
+        pushes.append(pltpu.make_async_copy(buf.at[part], dst_ref.at[part], out_sem.at[i]))
+    for copy in pulls:
+        copy.start()
+    for pull, push in zip(pulls, pushes):
+        pull.wait()
+        push.start()
+    for copy in pushes:
+        copy.wait()
+
+
+def settle(result, pieces):
+    hbm = pl.BlockSpec(memory_space=pl.ANY)
+    dma = pltpu.SemaphoreType.DMA
+    return pl.pallas_call(
+        settle_kernel,
+        out_shape=jax.ShapeDtypeStruct(result.shape, result.dtype),
+        in_specs=[hbm],
+        out_specs=hbm,
+        scratch_shapes=[pltpu.VMEM(result.shape, result.dtype), dma((pieces,)), dma((pieces,))],
+        compiler_params=pltpu.CompilerParams(vmem_limit_bytes=VMEM_LIMIT),
+        cost_estimate=pl.CostEstimate(flops=0, bytes_accessed=4 * result.size, transcendentals=0),
+    )(result)
+
+
 def per_device_kernel(groups, members, orbitals, projectors, coupling, species, offsets):
     chunks = orbitals.shape[0] // (groups * TILE)
-    return fused(
+    result = fused(
         chunks, members, orbitals, projectors, jnp.transpose(coupling, (1, 0, 2)), species[None, :], offsets[None, :]
     )
+    return settle(result, 2 * chunks)
 
 
 def per_device_plain(orbitals, projectors, coupling, species, offsets):

time: 119 us -> 114 us (0.958)
  local copies, waits for them, and re-layouts: 6.02 us -> 0 us
    unnamed x1 -> x0, local copies, waits for them, and re-layouts: 6.02 us -> none
    pallas_call x0 -> x1, Pallas kernels: none -> 2.39 us  [settle(): pl.pallas_call(settle_kernel, out_shape=jax.ShapeDtypeStruct(result.shape...]
    pallas_call x1, Pallas kernels: 113 us -> 111 us  [fused(): pl.pallas_call(functools.partial(kernel, chunks), out_shape=jax.ShapeDtyp...]
where the time goes in v3:
time: 114 us
  Pallas kernels  114 us (100%)
    pallas_call x1, Pallas kernels, fused(): pl.pallas_call(functools.partial(kernel, chunks), out_shape=jax.ShapeDtyp...  111 us
    pallas_call x1, Pallas kernels, settle(): pl.pallas_call(settle_kernel, out_shape=jax.ShapeDtypeStruct(result.shape...  2.39 us

profile of v3, /device:TPU:1, one launch (start us, length us, event | category | flops | bytes accessed | tf_op | source)
XLA Modules:
  0.0 114.0 jit_solution(17778140976140224729)
XLA Ops:
  0.0 111.4 %shard_map.55.src_ref = bf16[64,2,8192]{2,1,0:T(2,128)(2,1)} custom-call(bf16[64,2,8192]{2,1,0:T(2,128)(2,1)} %o_ref.1, bf16[864,2,512]{2,1,0:T(2,128)(2,1)} %p_ref.1, f32[18,4,18]{2,1,0:T(4,128)} %bitcast.3, s32[1,48]{1,0:T(1,128)} %bitcast.4, s32[1,48]{1,0:T(1,128)} %bitcast.5), custom_call_target="tpu_custom_call" | custom-call | flops 15032385536 | bytes 4194304 | tf_op jit(solution)/shard_map/pallas_call | solution.py:363
  111.5 2.4 %shard_map.56 = bf16[64,2,8192]{2,1,0:T(2,128)(2,1)} custom-call(bf16[64,2,8192]{2,1,0:T(2,128)(2,1)} %shard_map.55.src_ref), custom_call_target="tpu_custom_call" | custom-call | bytes 4194304 | tf_op jit(solution)/shard_map/pallas_call | solution.py:420

commit v4 on v3

--- a/solution.py
+++ b/solution.py
@@ -20,7 +20,7 @@
 DELAYS = (
     (12, 16, 20, 24, 28),
     (12, 16, 20, 24, 28),
-    (12, 16, 20, 24, 28),
+    (12, 16, 20, 25, 28),
     (12, 17, 20, 24, 28),
 )
 

time: 114 us -> 114 us (level)
  no operation moved by 1% of the time
where the time goes in v4:
time: 114 us
  Pallas kernels  114 us (100%)
    pallas_call x1, Pallas kernels, fused(): pl.pallas_call(functools.partial(kernel, chunks), out_shape=jax.ShapeDtyp...  111 us
    pallas_call x1, Pallas kernels, settle(): pl.pallas_call(settle_kernel, out_shape=jax.ShapeDtypeStruct(result.shape...  2.39 us

profile of v4, /device:TPU:1, one launch (start us, length us, event | category | flops | bytes accessed | tf_op | source)
XLA Modules:
  0.0 113.9 jit_solution(5966668630654620288)
XLA Ops:
  0.0 111.3 %shard_map.55.src_ref = bf16[64,2,8192]{2,1,0:T(2,128)(2,1)} custom-call(bf16[64,2,8192]{2,1,0:T(2,128)(2,1)} %o_ref.1, bf16[864,2,512]{2,1,0:T(2,128)(2,1)} %p_ref.1, f32[18,4,18]{2,1,0:T(4,128)} %bitcast.3, s32[1,48]{1,0:T(1,128)} %bitcast.4, s32[1,48]{1,0:T(1,128)} %bitcast.5), custom_call_target="tpu_custom_call" | custom-call | flops 15032385536 | bytes 4194304 | tf_op jit(solution)/shard_map/pallas_call | solution.py:363
  111.4 2.4 %shard_map.56 = bf16[64,2,8192]{2,1,0:T(2,128)(2,1)} custom-call(bf16[64,2,8192]{2,1,0:T(2,128)(2,1)} %shard_map.55.src_ref), custom_call_target="tpu_custom_call" | custom-call | bytes 4194304 | tf_op jit(solution)/shard_map/pallas_call | solution.py:420
